TPU v7x, 32 devices: a whole 2x2x4 slice. The times are simulated.
32 devices in a mesh: gx: 8 (over z, x), gy: 4 (over y, core).
Axes of the slice: x: 2, y: 2, z: 4, core: 2. Of those that a mesh axis runs over, the one named last changes fastest.
Arguments:
- dense_grads: float32 [32, 256, 1024], P(('gx', 'gy')), may hold values from -6 to 6
- dense_param: float32 [256, 1024], P(('gx', 'gy')), may hold values from -6 to 6
- dense_acc: float32 [256, 1024], P(('gx', 'gy'))
- table: float32 [131072, 128], P(('gx', 'gy')), may hold values from -6 to 6
- row_acc: float32 [131072], P(('gx', 'gy'))
- touched: int32 [16384], P(('gx', 'gy')), may hold values from 0 to 4095, as said below
- emb_grads: float32 [16384, 128], P(('gx', 'gy'))
Outputs:
- new_dense: float32 [256, 1024], P(('gx', 'gy'))
- new_dense_acc: float32 [256, 1024], P(('gx', 'gy'))
- new_table: float32 [131072, 128], P(('gx', 'gy'))
- new_row_acc: float32 [131072], P(('gx', 'gy'))
Inputs may be any that keep to these rules, and one draw needn't show every extreme that they name: `touched`: within one device's 512 entries no row number repeats.
All inputs are finite; a program needn't handle non-finite values.
Results may differ from a plain program's by a relative error of at most 0.000022.
Values sent between devices are 32-bit elements; how exact they have to be, the bound alone decides.
No kernel may reach another device: no remote copies, remote signals or barrier semaphores. Data moves between devices by JAX's collectives and lax.ppermute only.
A program may use at most 128 MiB of HBM per device.

v0:
```python
import jax
import jax.numpy as jnp
from jax import lax
from jax.sharding import PartitionSpec as P

learn_rate = 0.5
max_norm = 8.0
epsilon = 1e-10


def body(dense_grads, dense_param, dense_acc, table, row_acc, touched, emb_grads):
    shards = lax.axis_size(("gx", "gy"))
    local_grad = dense_grads[0]
    embed_square = jnp.sum(emb_grads * emb_grads)
    own_rows = dense_param.shape[0]
    summed, embed_total = lax.psum((local_grad, embed_square), ("gx", "gy"))
    mean_whole = summed / jnp.float32(shards)
    norm_sq = jnp.sum(mean_whole * mean_whole) + embed_total
    start = lax.axis_index(("gx", "gy")) * own_rows
    mean_grad = lax.dynamic_slice_in_dim(mean_whole, start, own_rows, 0)
    clip = jnp.minimum(jnp.float32(1.0), max_norm / (jnp.sqrt(norm_sq) + 1e-06))
    scaled = clip * mean_grad
    new_dense_acc = dense_acc + scaled * scaled
    new_dense = dense_param - learn_rate * scaled / (jnp.sqrt(new_dense_acc) + epsilon)
    row_grads = clip * emb_grads
    square_mean = jnp.mean(row_grads * row_grads, axis=1)
    updated_acc = row_acc[touched] + square_mean
    new_row_acc = row_acc.at[touched].set(updated_acc)
    updated_rows = (
        table[touched] - learn_rate * row_grads / (jnp.sqrt(updated_acc) + epsilon)[:, None]
    )
    new_table = table.at[touched].set(updated_rows)
    return (new_dense, new_dense_acc, new_table, new_row_acc)


def solution(mesh):
    return jax.shard_map(
        body,
        mesh=mesh,
        in_specs=(
            P(("gx", "gy"), None, None),
            P(("gx", "gy"), None),
            P(("gx", "gy"), None),
            P(("gx", "gy"), None),
            P(("gx", "gy")),
            P(("gx", "gy")),
            P(("gx", "gy"), None),
        ),
        out_specs=(
            P(("gx", "gy"), None),
            P(("gx", "gy"), None),
            P(("gx", "gy"), None),
            P(("gx", "gy")),
        ),
        check_vma=False,
    )
```

profile of v0, /device:TPU:0, one launch (start us, length us, event | category | flops | bytes accessed | tf_op | source)
XLA Modules:
  0.0 165.0 jit_solution(8833698111364106730)
XLA Ops:
  7.2 0.0 all-reduce.2.cloned.1.call-start
  7.2 0.7 copy.18
  7.9 0.0 all-reduce.2.cloned.1.call-update
  8.0 0.9 copy-done.3
  8.9 0.7 multiply_reduce_fusion.2
  9.5 42.3 %psum.15 = f32[]{:T(128)} all-reduce(f32[]{:T(128)} %multiply_reduce_fusion.2), channel_id=1, replica_groups=mesh['gx'=8,'gy'=4] {'gx','gy'}, use_global_device_ids=true, to_apply=%region_3.0 | all-reduce | flops 1 | bytes 8 | tf_op jit(solution)/shard_map/psum | solution.py:16
  51.9 0.0 copy-done.6
  51.9 3.1 %gather_fusion = f32[512]{0:T(512)S(1)} fusion(f32[4096]{0:T(1024)S(1)} %copy.18, s32[1024]{0:T(1024)S(1)} %pad_clamp_fusion), kind=kCustom, calls=%fused_computation.1 | custom fusion | bytes 6144 | tf_op jit(solution)/shard_map/gather | solution.py:27
  55.0 91.9 %all-reduce.2.cloned.1.call-done = f32[256,1024]{1,0:T(8,128)} async-done(((f32[256,1024]{1,0:T(8,128)}), f32[256,1024]{1,0:T(8,128)}) %all-reduce.2.cloned.1.call-update) | async-done | bytes 1048592 | tf_op jit(solution)/shard_map/psum | solution.py:16
  147.0 2.1 %multiply_reduce_fusion = (f32[]{:T(128)}, f32[256,1024]{1,0:T(8,128)S(1)}) fusion(f32[256,1024]{1,0:T(8,128)} %all-reduce.2.cloned.1.call-done), kind=kLoop, calls=%fused_computation.4 | loop fusion | flops 786431 | bytes 2097156 | tf_op jit(solution)/shard_map/reduce_sum | solution.py:18
  150.5 0.1 multiply_reduce_fusion.1
  150.6 0.0 copy-start.2
  150.6 2.5 %scatter_fusion = f32[4096]{0:T(1024)S(1)} fusion(f32[4096]{0:T(1024)S(1)} %copy.18, s32[512]{0:T(512)S(1)} %compare_select_fusion, f32[512]{0:T(512)S(1)} %get-tuple-element.5), kind=kCustom, calls=%fused_computation.3 | custom fusion | bytes 8192 | tf_op jit(solution)/shard_map/scatter | solution.py:28
  153.1 0.0 copy-start
  153.1 0.0 copy-done.2
  153.1 0.0 copy-start.4
  153.2 0.0 copy-start.5
  153.2 3.6 %scatter_custom_fusion = f32[4096,128]{1,0:T(8,128)S(1)} fusion(f32[4096,128]{1,0:T(8,128)S(1)} %copy-done.2, s32[512]{0:T(512)S(1)} %compare_select_fusion, f32[512,128]{1,0:T(8,128)S(1)} %copy-done.3, f32[512]{0:T(512)S(1)} %get-tuple-element.4, f32[]{:T(128)} %constant.14.clone.1, f32[]{:T(128)S(6)} %min_shard_map.3, s32[1024]{0:T(1024)S(1)} %pad_clamp_fusion), kind=kCustom, calls=%fused_computation.6 | custom fusion | flops 262144 | bytes 4462600 | tf_op jit(solution)/shard_map/scatter | solution.py:32
  156.8 0.0 copy-done
  156.8 0.0 copy-start.1
  156.8 0.0 copy-done.4
  156.8 0.0 copy-done.5
  156.8 0.8 divide_subtract_fusion
  157.6 0.5 copy-done.1
  (5 shorter events, 0.0 us)
Async XLA Ops:
  7.2 139.8 %all-reduce.2.cloned.1.call-start = ((), (), s32[]{:S(2)}) async-start(), calls=%async_computation | async-start | bytes 2097152 | tf_op jit(solution)/shard_map/psum | solution.py:16
  7.9 0.9 copy-start.3
  7.9 43.9 %copy-start.6 = (s32[512]{0:T(512)S(1)}, s32[512]{0:T(512)}, u32[]{:S(2)}) copy-start(s32[512]{0:T(512)} %param.12) | copy-start | bytes 6148
  150.6 2.5 %copy-start.2 = (f32[4096,128]{1,0:T(8,128)S(1)}, f32[4096,128]{1,0:T(8,128)}, u32[]{:S(2)}) copy-start(f32[4096,128]{1,0:T(8,128)} %param.10) | copy-start | bytes 6291460
  153.1 3.7 %copy-start = (f32[4096]{0:T(1024)}, f32[4096]{0:T(1024)S(1)}, u32[]{:S(2)}) copy-start(f32[4096]{0:T(1024)S(1)} %scatter_fusion) | copy-start | bytes 49156
  153.1 3.7 %copy-start.4 = (f32[8,1024]{1,0:T(8,128)S(1)}, f32[8,1024]{1,0:T(8,128)}, u32[]{:S(2)}) copy-start(f32[8,1024]{1,0:T(8,128)} %param.8) | copy-start | bytes 98308
  153.2 3.7 %copy-start.5 = (f32[8,1024]{1,0:T(8,128)S(1)}, f32[8,1024]{1,0:T(8,128)}, u32[]{:S(2)}) copy-start(f32[8,1024]{1,0:T(8,128)} %param.9) | copy-start | bytes 98308
  156.8 1.3 copy-start.1
Sparse Core Ops, SparseCore 0:
  13.2 133.7 all-reduce.1
where the time goes:
time: 165 us
  waiting for transfers between devices  92 us (56%)
  blocking collectives  42.3 us (26%)
  between operations  15.5 us (9%)
  local copies, waits for them, and re-layouts  7.84 us (5%)
  other arithmetic  7.32 us (4%)
    psum x1, waiting for transfers between devices, body(): summed, embed_total = lax.psum((local_grad, embed_square), ('gx', 'gy'))  91.9 us
    psum x1, blocking collectives, body(): summed, embed_total = lax.psum((local_grad, embed_square), ('gx', 'gy'))  42.3 us
    scatter x1, other arithmetic, body(): new_table = table.at[touched].set(updated_rows)  3.6 us
  transfers between devices with their start and end apart: 1, of which 1 were waited for; matrix products, arithmetic and copies ran while one was open for 2% of the time, Pallas kernels for 0%

commit v1 on v0

v1 whole, which is shorter than its diff:
```python
import jax
import jax.numpy as jnp
from jax import lax
from jax.sharding import PartitionSpec as P

learn_rate = 0.5
max_norm = 8.0
epsilon = 1e-10
axes = ("gx", "gy")
lanes = 128


def swap(value, mask):
    count = lax.axis_size(axes)
    return lax.ppermute(value, axes, [(i, i ^ mask) for i in range(count)])


def pick(value, live, bits, flip):
    index = lax.axis_index(axes)
    for bit in bits:
        chosen = (index >> bit) & 1
        if (flip >> bit) & 1:
            chosen = 1 - chosen
        value = lax.dynamic_index_in_dim(value, chosen, live.index(bit), keepdims=False)
        live = [other for other in live if other != bit]
    return value


def reduced(local_grad, embed_square):
    count = lax.axis_size(axes)
    total_bits = count.bit_length() - 1
    own_rows = local_grad.shape[0] // count
    width = local_grad.shape[1]
    data = local_grad.reshape((2,) * total_bits + (own_rows, width))
    live = list(range(total_bits))[::-1]
    last = list(range(max(total_bits - 2, 3), total_bits))
    rounds = [[0], [1, 2]] + [[bit] for bit in range(3, last[0])]
    for bits in rounds:
        masks = [sum(((code >> j) & 1) << bit for j, bit in enumerate(bits)) for code in range(1, 2 ** len(bits))]
        arrived = [swap(pick(data, live, bits, mask), mask) for mask in masks[::-1]]
        data = pick(data, live, bits, 0)
        for part in arrived:
            data = data + part
        live = [bit for bit in live if bit not in bits]
    lead = data.shape[:-2]
    tile = jnp.zeros(lead + (own_rows, lanes), jnp.float32)
    tile = tile.at[(0,) * len(lead)].set(embed_square)
    data = jnp.concatenate([data, tile], axis=-1)
    for bit in last:
        data = data + swap(data, 1 << bit)
    mean = data[..., :width] / jnp.float32(count)
    squares = jnp.sum(jnp.square(mean).reshape((-1, own_rows, width // lanes, lanes)), axis=(0, 2))
    partial = squares + data[..., width:][(0,) * len(lead)]
    for bit in [bit for bits in rounds[::-1] for bit in bits]:
        partial = partial + swap(partial, 1 << bit)
    return pick(mean, live, live, 0), partial


def body(dense_grads, dense_param, dense_acc, table, row_acc, touched, emb_grads):
    own_rows = dense_param.shape[0]
    square = emb_grads * emb_grads
    embed_square = jnp.sum(square.reshape((-1, own_rows, emb_grads.shape[1])), axis=0)
    row_square = jnp.mean(square, axis=1)
    square_table = jnp.zeros_like(row_acc).at[touched].set(row_square, unique_indices=True)
    old_acc = row_acc[touched]
    old_rows = table[touched]

    mean_grad, partial = reduced(dense_grads[0], embed_square)
    norm_sq = jnp.sum(partial)
    clip = jnp.minimum(jnp.float32(1.0), max_norm / (jnp.sqrt(norm_sq) + 1e-06))
    scaled = clip * mean_grad
    new_dense_acc = dense_acc + scaled * scaled
    new_dense = dense_param - learn_rate * scaled / (jnp.sqrt(new_dense_acc) + epsilon)
    clip_sq = clip * clip
    new_row_acc = row_acc + jnp.where(clip > 0, clip_sq * square_table, 0.0)
    updated_acc = old_acc + jnp.where(clip > 0, clip_sq * row_square, 0.0)
    updated_rows = old_rows - learn_rate * (clip * emb_grads) / (jnp.sqrt(updated_acc) + epsilon)[:, None]
    new_table = table.at[touched].set(updated_rows, unique_indices=True)
    return (new_dense, new_dense_acc, new_table, new_row_acc)


def solution(mesh):
    return jax.shard_map(
        body,
        mesh=mesh,
        in_specs=(
            P(axes, None, None),
            P(axes, None),
            P(axes, None),
            P(axes, None),
            P(axes),
            P(axes),
            P(axes, None),
        ),
        out_specs=(P(axes, None), P(axes, None), P(axes, None), P(axes)),
        check_vma=False,
    )
```

time: 165 us -> 48.6 us (0.29)
  waiting for transfers between devices: 92 us -> 21.3 us
  blocking collectives: 42.3 us -> 0 us
  between operations: 15.5 us -> 1.58 us
  starting transfers between devices: 0.04 us -> 12.1 us
    psum x1 -> x0, waiting for transfers between devices: 91.9 us -> none  [body(): summed, embed_total = lax.psum((local_grad, embed_square), ('gx', 'gy'))]
    psum x1 -> x0, blocking collectives: 42.3 us -> none  [body(): summed, embed_total = lax.psum((local_grad, embed_square), ('gx', 'gy'))]
    ppermute x0 -> x9, waiting for transfers between devices: none -> 21.3 us  [swap(): return lax.ppermute(value, axes, [(i, i ^ mask) for i in range(count)])]
    ppermute x0 -> x9, starting transfers between devices: none -> 12.1 us  [swap(): return lax.ppermute(value, axes, [(i, i ^ mask) for i in range(count)])]
    reduce_sum x3 -> x5, other arithmetic: 2.92 us -> 0.84 us  [the longest x1 0.6 us: body(): norm_sq = jnp.sum(partial)]
  transfers between devices with their start and end apart: 1 -> 9, of which waited for: 1 -> 8; matrix products, arithmetic and copies ran while one was open for 2% -> 7% of each run, Pallas kernels for 0% -> 0%
where the time goes in v1:
time: 48.6 us; the launch traced here: 48.5 us
  waiting for transfers between devices  21.3 us (44%)
  starting transfers between devices  12.1 us (25%)
  local copies, waits for them, and re-layouts  7.6 us (16%)
  other arithmetic  5.96 us (12%)
  between operations  1.58 us (3%)
    ppermute x9, waiting for transfers between devices, swap(): return lax.ppermute(value, axes, [(i, i ^ mask) for i in range(count)])  21.3 us
    ppermute x9, starting transfers between devices, swap(): return lax.ppermute(value, axes, [(i, i ^ mask) for i in range(count)])  12.1 us
    scatter x1, other arithmetic, body(): new_table = table.at[touched].set(updated_rows, unique_indices=True)  3.6 us
    gather x1, local copies, waits for them, and re-layouts, body(): old_acc = row_acc[touched]  3.14 us
    scatter x1, local copies, waits for them, and re-layouts, body(): jnp.zeros_like(row_acc).at[touched].set(row_square, unique_indices=True)  2.46 us
    unnamed x16, local copies, waits for them, and re-layouts  1.81 us
  transfers between devices with their start and end apart: 9, of which 8 were waited for; matrix products, arithmetic and copies ran while one was open for 7% of the time, Pallas kernels for 0%

profile of v1, /device:TPU:0, one launch (start us, length us, event | category | flops | bytes accessed | tf_op | source)
XLA Modules:
  0.0 48.5 jit_solution(11962329479371246906)
XLA Ops:
  0.6 1.2 %copy-done.4 = f32[1,256,1024]{2,1,0:T(8,128)S(1)} copy-done((f32[1,256,1024]{2,1,0:T(8,128)S(1)}, f32[1,256,1024]{2,1,0:T(8,128)}, u32[]{:S(2)}) %copy-start.4) | copy-done | bytes 1048600
  2.0 0.6 %collective-permute-start = (f32[2,2,2,2,8,1024]{5,4,1,0,3,2:T(8,128)S(1)}, f32[2,2,2,2,8,1024]{5,4,1,0,3,2:T(8,128)S(1)}, u32[]{:S(2)}, u32[]{:S(2)}) collective-permute-start(f32[2,2,2,2,8,1024]{5,4,1,0,3,2:T(8,128)S(1)} %bitcast.35), channel_id=1, source_target_pairs={{0,1},{1,0},{2,3},{3,2},{4,5},{5,4},{6,7},{7,6},{8,9},{9,8},{10,11... | collective-permute-start | bytes 1572872 | tf_op jit(solution)/shard_map/ppermute | solution.py:15
  2.6 1.5 %collective-permute-done = f32[2,2,2,2,8,1024]{5,4,1,0,3,2:T(8,128)S(1)} collective-permute-done((f32[2,2,2,2,8,1024]{5,4,1,0,3,2:T(8,128)S(1)}, f32[2,2,2,2,8,1024]{5,4,1,0,3,2:T(8,128)S(1)}, u32[]{:S(2)}, u32[]{:S(2)}) %collective-permute-start) | collective-permute-done | bytes 524320 | tf_op jit(solution)/shard_map/ppermute | solution.py:15
  4.2 2.9 %collective-permute-start.3 = (f32[2,2,8,1024]{3,2,1,0:T(8,128)S(1)}, f32[2,2,8,1024]{3,2,1,0:T(8,128)S(1)}, u32[]{:S(2)}, u32[]{:S(2)}) collective-permute-start(f32[2,2,8,1024]{3,2,1,0:T(8,128)S(1)} %get-tuple-element.21), channel_id=1, source_target_pairs={{0,2},{1,3},{2,0},{3,1},{4,6},{5,7},{6,4},{7,5},{8,10},{9,11},{10,... | collective-permute-start | bytes 393224 | tf_op jit(solution)/shard_map/ppermute | solution.py:15
  7.2 1.5 %collective-permute-start.2 = (f32[2,2,8,1024]{3,2,1,0:T(8,128)S(1)}, f32[2,2,8,1024]{3,2,1,0:T(8,128)S(1)}, u32[]{:S(2)}, u32[]{:S(2)}) collective-permute-start(f32[2,2,8,1024]{3,2,1,0:T(8,128)S(1)} %get-tuple-element.22), channel_id=1, source_target_pairs={{0,4},{1,5},{2,6},{3,7},{4,0},{5,1},{6,2},{7,3},{8,12},{9,13},{10,... | collective-permute-start | bytes 393224 | tf_op jit(solution)/shard_map/ppermute | solution.py:15
  8.8 2.2 %collective-permute-done.3 = f32[2,2,8,1024]{3,2,1,0:T(8,128)S(1)} collective-permute-done((f32[2,2,8,1024]{3,2,1,0:T(8,128)S(1)}, f32[2,2,8,1024]{3,2,1,0:T(8,128)S(1)}, u32[]{:S(2)}, u32[]{:S(2)}) %collective-permute-start.3) | collective-permute-done | bytes 131104 | tf_op jit(solution)/shard_map/ppermute | solution.py:15
  11.0 2.6 %collective-permute-done.2 = f32[2,2,8,1024]{3,2,1,0:T(8,128)S(1)} collective-permute-done((f32[2,2,8,1024]{3,2,1,0:T(8,128)S(1)}, f32[2,2,8,1024]{3,2,1,0:T(8,128)S(1)}, u32[]{:S(2)}, u32[]{:S(2)}) %collective-permute-start.2) | collective-permute-done | bytes 131104 | tf_op jit(solution)/shard_map/ppermute | solution.py:15
  13.6 1.5 %collective-permute-done.1 = f32[2,2,8,1024]{3,2,1,0:T(8,128)S(1)} collective-permute-done((f32[2,2,8,1024]{3,2,1,0:T(8,128)S(1)}, f32[2,2,8,1024]{3,2,1,0:T(8,128)S(1)}, u32[]{:S(2)}, u32[]{:S(2)}) %collective-permute-start.1) | collective-permute-done | bytes 131104 | tf_op jit(solution)/shard_map/ppermute | solution.py:15
  15.1 1.8 %collective-permute-start.4 = (f32[2,2,8,1152]{3,2,1,0:T(8,128)S(1)}, f32[2,2,8,1152]{3,2,1,0:T(8,128)S(1)}, u32[]{:S(2)}, u32[]{:S(2)}) collective-permute-start(f32[2,2,8,1152]{3,2,1,0:T(8,128)S(1)} %select_maximum_fusion), channel_id=1, source_target_pairs={{0,8},{1,9},{2,10},{3,11},{4,12},{5,13},{6,14},{7,15},{8,0},{9,1},... | collective-permute-start | bytes 442376 | tf_op jit(solution)/shard_map/ppermute | solution.py:15
  16.9 3.4 %collective-permute-done.4 = f32[2,2,8,1152]{3,2,1,0:T(8,128)S(1)} collective-permute-done((f32[2,2,8,1152]{3,2,1,0:T(8,128)S(1)}, f32[2,2,8,1152]{3,2,1,0:T(8,128)S(1)}, u32[]{:S(2)}, u32[]{:S(2)}) %collective-permute-start.4) | collective-permute-done | bytes 147488 | tf_op jit(solution)/shard_map/ppermute | solution.py:15
  20.3 2.8 %collective-permute-start.5 = (f32[2,2,8,1152]{3,2,1,0:T(8,128)S(1)}, f32[2,2,8,1152]{3,2,1,0:T(8,128)S(1)}, u32[]{:S(2)}, u32[]{:S(2)}) collective-permute-start(f32[2,2,8,1152]{3,2,1,0:T(8,128)S(1)} %fusion.15), channel_id=1, source_target_pairs={{0,16},{1,17},{2,18},{3,19},{4,20},{5,21},{6,22},{7,23},{8,24},{9,... | collective-permute-start | bytes 442376 | tf_op jit(solution)/shard_map/ppermute | solution.py:15
  23.1 5.4 %collective-permute-done.5 = f32[2,2,8,1152]{3,2,1,0:T(8,128)S(1)} collective-permute-done((f32[2,2,8,1152]{3,2,1,0:T(8,128)S(1)}, f32[2,2,8,1152]{3,2,1,0:T(8,128)S(1)}, u32[]{:S(2)}, u32[]{:S(2)}) %collective-permute-start.5) | collective-permute-done | bytes 147488 | tf_op jit(solution)/shard_map/ppermute | solution.py:15
  28.6 1.3 %collective-permute-start.6 = (f32[8,128]{1,0:T(8,128)S(1)}, f32[8,128]{1,0:T(8,128)S(1)}, u32[]{:S(2)}, u32[]{:S(2)}) collective-permute-start(f32[8,128]{1,0:T(8,128)S(1)} %fusion.13), channel_id=1, source_target_pairs={{0,2},{1,3},{2,0},{3,1},{4,6},{5,7},{6,4},{7,5},{8,10},{9,11},{10,... | collective-permute-start | bytes 12296 | tf_op jit(solution)/shard_map/ppermute | solution.py:15
  29.9 2.4 %collective-permute-done.6 = f32[8,128]{1,0:T(8,128)S(1)} collective-permute-done((f32[8,128]{1,0:T(8,128)S(1)}, f32[8,128]{1,0:T(8,128)S(1)}, u32[]{:S(2)}, u32[]{:S(2)}) %collective-permute-start.6) | collective-permute-done | bytes 4128 | tf_op jit(solution)/shard_map/ppermute | solution.py:15
  32.3 1.2 %collective-permute-start.7 = (f32[8,128]{1,0:T(8,128)S(1)}, f32[8,128]{1,0:T(8,128)S(1)}, u32[]{:S(2)}, u32[]{:S(2)}) collective-permute-start(f32[8,128]{1,0:T(8,128)S(1)} %add.159), channel_id=1, source_target_pairs={{0,4},{1,5},{2,6},{3,7},{4,0},{5,1},{6,2},{7,3},{8,12},{9,13},{10,... | collective-permute-start | bytes 12296 | tf_op jit(solution)/shard_map/ppermute | solution.py:15
  33.5 0.1 multiply_reduce_fusion
  33.6 2.3 %collective-permute-done.7 = f32[8,128]{1,0:T(8,128)S(1)} collective-permute-done((f32[8,128]{1,0:T(8,128)S(1)}, f32[8,128]{1,0:T(8,128)S(1)}, u32[]{:S(2)}, u32[]{:S(2)}) %collective-permute-start.7) | collective-permute-done | bytes 4128 | tf_op jit(solution)/shard_map/ppermute | solution.py:15
  35.9 3.1 %gather_fusion = f32[512]{0:T(512)S(1)} fusion(f32[4096]{0:T(1024)S(1)} %copy-done, s32[1024]{0:T(1024)S(1)} %pad_clamp_fusion), kind=kCustom, calls=%fused_computation.1 | custom fusion | bytes 6144 | tf_op jit(solution)/shard_map/gather | solution.py:65
  39.1 0.6 %add_reduce_fusion = f32[]{:T(128)} fusion(f32[8,128]{1,0:T(8,128)S(1)} %add.160, f32[8,128]{1,0:T(8,128)S(1)} %collective-permute-done.8), kind=kLoop, calls=%fused_computation.38 | loop fusion | flops 2047 | bytes 8196 | tf_op jit(solution)/shard_map/reduce_sum | solution.py:69
  40.4 2.5 %scatter_custom_fusion.1 = f32[4096]{0:T(1024)S(1)} fusion(s32[512]{0:T(512)S(1)} %compare_select_fusion, f32[512]{0:T(512)S(1)} %get-tuple-element.25, f32[]{:T(128)} %constant.233.clone.1), kind=kCustom, calls=%fused_computation.32 | custom fusion | bytes 16388 | tf_op jit(solution)/shard_map/scatter | solution.py:64
  42.9 0.6 %select_add_fusion = f32[4096]{0:T(1024)} fusion(f32[4096]{0:T(1024)S(1)} %copy-done, f32[4096]{0:T(1024)S(1)} %scatter_custom_fusion.1, f32[]{:T(128)S(6)} %mul.80, pred[]{:T(512)S(6)} %gt.4), kind=kLoop, calls=%fused_computation.31 | loop fusion | flops 12288 | bytes 49157 | tf_op jit(solution)/shard_map/add | solution.py:75
  43.5 3.6 %scatter_custom_fusion = f32[4096,128]{1,0:T(8,128)S(1)} fusion(f32[4096,128]{1,0:T(8,128)S(1)} %copy-done.2, s32[512]{0:T(512)S(1)} %compare_select_fusion, f32[512,128]{1,0:T(8,128)S(1)} %copy-done.3, f32[512]{0:T(512)S(1)} %get-tuple-element.26, f32[]{:T(128)} %constant.237.clone.1, f32[]{:T(128)S(6)} %min_shard_map.3, s32[1024]{0:T(1024)S(1)} %pad_clamp_fusion), kind=kCustom, calls=%fused_computation.7 | custom fusion | flops 262144 | bytes 4462600 | tf_op jit(solution)/shard_map/scatter | solution.py:78
  47.2 0.7 %fusion.10 = (f32[8,1024]{1,0:T(8,128)}, f32[8,1024]{1,0:T(8,128)}) fusion(f32[8,1024]{1,0:T(8,128)S(1)} %copy-done.5, f32[2,2,8,1024]{3,2,1,0:T(8,128)S(1)} %get-tuple-element.24, s32[]{:T(128)S(6)} %select_n.82, s32[]{:T(128)S(6)} %select_n.84, f32[]{:T(128)S(6)} %min_shard_map.3, f32[8,1024]{1,0:T(8,128)S(1)} %copy-done.6), kind=kLoop, calls=%fused_computation.28 | loop fusion | flops 57344 | bytes 163852 | tf_op jit(solution)/shard_map/sub | solution.py:73
  47.9 0.6 %copy-done.1 = f32[4096,128]{1,0:T(8,128)} copy-done((f32[4096,128]{1,0:T(8,128)}, f32[4096,128]{1,0:T(8,128)S(1)}, u32[]{:S(2)}) %copy-start.1) | copy-done | bytes 2097176
  (34 shorter events, 0.5 us)
Async XLA Ops:
  0.6 1.2 %copy-start.4 = (f32[1,256,1024]{2,1,0:T(8,128)S(1)}, f32[1,256,1024]{2,1,0:T(8,128)}, u32[]{:S(2)}) copy-start(f32[1,256,1024]{2,1,0:T(8,128)} %param.9) | copy-start | bytes 3145732
  2.0 6.8 %copy-start.3 = (f32[512,128]{1,0:T(8,128)S(1)}, f32[512,128]{1,0:T(8,128)}, u32[]{:S(2)}) copy-start(f32[512,128]{1,0:T(8,128)} %param.15) | copy-start | bytes 786436
  2.0 2.1 %collective-permute-start = (f32[2,2,2,2,8,1024]{5,4,1,0,3,2:T(8,128)S(1)}, f32[2,2,2,2,8,1024]{5,4,1,0,3,2:T(8,128)S(1)}, u32[]{:S(2)}, u32[]{:S(2)}) collective-permute-start(f32[2,2,2,2,8,1024]{5,4,1,0,3,2:T(8,128)S(1)} %bitcast.35), channel_id=1, source_target_pairs={{0,1},{1,0},{2,3},{3,2},{4,5},{5,4},{6,7},{7,6},{8,9},{9,8},{10,11... | collective-permute-start | bytes 1572872 | tf_op jit(solution)/shard_map/ppermute | solution.py:15
  4.1 25.8 %copy-start.7 = (s32[512]{0:T(512)S(1)}, s32[512]{0:T(512)}, u32[]{:S(2)}) copy-start(s32[512]{0:T(512)} %param.14) | copy-start | bytes 6148
  4.2 31.7 %copy-start = (f32[4096]{0:T(1024)S(1)}, f32[4096]{0:T(1024)}, u32[]{:S(2)}) copy-start(f32[4096]{0:T(1024)} %param.13) | copy-start | bytes 49156
  4.2 6.7 %collective-permute-start.3 = (f32[2,2,8,1024]{3,2,1,0:T(8,128)S(1)}, f32[2,2,8,1024]{3,2,1,0:T(8,128)S(1)}, u32[]{:S(2)}, u32[]{:S(2)}) collective-permute-start(f32[2,2,8,1024]{3,2,1,0:T(8,128)S(1)} %get-tuple-element.21), channel_id=1, source_target_pairs={{0,2},{1,3},{2,0},{3,1},{4,6},{5,7},{6,4},{7,5},{8,10},{9,11},{10,... | collective-permute-start | bytes 393224 | tf_op jit(solution)/shard_map/ppermute | solution.py:15
  7.2 6.4 %collective-permute-start.2 = (f32[2,2,8,1024]{3,2,1,0:T(8,128)S(1)}, f32[2,2,8,1024]{3,2,1,0:T(8,128)S(1)}, u32[]{:S(2)}, u32[]{:S(2)}) collective-permute-start(f32[2,2,8,1024]{3,2,1,0:T(8,128)S(1)} %get-tuple-element.22), channel_id=1, source_target_pairs={{0,4},{1,5},{2,6},{3,7},{4,0},{5,1},{6,2},{7,3},{8,12},{9,13},{10,... | collective-permute-start | bytes 393224 | tf_op jit(solution)/shard_map/ppermute | solution.py:15
  8.7 6.4 %collective-permute-start.1 = (f32[2,2,8,1024]{3,2,1,0:T(8,128)S(1)}, f32[2,2,8,1024]{3,2,1,0:T(8,128)S(1)}, u32[]{:S(2)}, u32[]{:S(2)}) collective-permute-start(f32[2,2,8,1024]{3,2,1,0:T(8,128)S(1)} %get-tuple-element.20), channel_id=1, source_target_pairs={{0,6},{1,7},{2,4},{3,5},{4,2},{5,3},{6,0},{7,1},{8,14},{9,15},{10,... | collective-permute-start | bytes 393224 | tf_op jit(solution)/shard_map/ppermute | solution.py:15
  15.1 28.4 %copy-start.2 = (f32[4096,128]{1,0:T(8,128)S(1)}, f32[4096,128]{1,0:T(8,128)}, u32[]{:S(2)}) copy-start(f32[4096,128]{1,0:T(8,128)} %param.12) | copy-start | bytes 6291460
  15.1 5.2 %collective-permute-start.4 = (f32[2,2,8,1152]{3,2,1,0:T(8,128)S(1)}, f32[2,2,8,1152]{3,2,1,0:T(8,128)S(1)}, u32[]{:S(2)}, u32[]{:S(2)}) collective-permute-start(f32[2,2,8,1152]{3,2,1,0:T(8,128)S(1)} %select_maximum_fusion), channel_id=1, source_target_pairs={{0,8},{1,9},{2,10},{3,11},{4,12},{5,13},{6,14},{7,15},{8,0},{9,1},... | collective-permute-start | bytes 442376 | tf_op jit(solution)/shard_map/ppermute | solution.py:15
  20.3 8.2 %collective-permute-start.5 = (f32[2,2,8,1152]{3,2,1,0:T(8,128)S(1)}, f32[2,2,8,1152]{3,2,1,0:T(8,128)S(1)}, u32[]{:S(2)}, u32[]{:S(2)}) collective-permute-start(f32[2,2,8,1152]{3,2,1,0:T(8,128)S(1)} %fusion.15), channel_id=1, source_target_pairs={{0,16},{1,17},{2,18},{3,19},{4,20},{5,21},{6,22},{7,23},{8,24},{9,... | collective-permute-start | bytes 442376 | tf_op jit(solution)/shard_map/ppermute | solution.py:15
  28.6 3.7 %collective-permute-start.6 = (f32[8,128]{1,0:T(8,128)S(1)}, f32[8,128]{1,0:T(8,128)S(1)}, u32[]{:S(2)}, u32[]{:S(2)}) collective-permute-start(f32[8,128]{1,0:T(8,128)S(1)} %fusion.13), channel_id=1, source_target_pairs={{0,2},{1,3},{2,0},{3,1},{4,6},{5,7},{6,4},{7,5},{8,10},{9,11},{10,... | collective-permute-start | bytes 12296 | tf_op jit(solution)/shard_map/ppermute | solution.py:15
  32.3 3.6 %collective-permute-start.7 = (f32[8,128]{1,0:T(8,128)S(1)}, f32[8,128]{1,0:T(8,128)S(1)}, u32[]{:S(2)}, u32[]{:S(2)}) collective-permute-start(f32[8,128]{1,0:T(8,128)S(1)} %add.159), channel_id=1, source_target_pairs={{0,4},{1,5},{2,6},{3,7},{4,0},{5,1},{6,2},{7,3},{8,12},{9,13},{10,... | collective-permute-start | bytes 12296 | tf_op jit(solution)/shard_map/ppermute | solution.py:15
  35.9 3.2 %collective-permute-start.8 = (f32[8,128]{1,0:T(8,128)S(1)}, f32[8,128]{1,0:T(8,128)S(1)}, u32[]{:S(2)}, u32[]{:S(2)}) collective-permute-start(f32[8,128]{1,0:T(8,128)S(1)} %add.160), channel_id=1, source_target_pairs={{0,1},{1,0},{2,3},{3,2},{4,5},{5,4},{6,7},{7,6},{8,9},{9,8},{10,11... | collective-permute-start | bytes 12296 | tf_op jit(solution)/shard_map/ppermute | solution.py:15
  43.5 3.6 %copy-start.5 = (f32[8,1024]{1,0:T(8,128)S(1)}, f32[8,1024]{1,0:T(8,128)}, u32[]{:S(2)}) copy-start(f32[8,1024]{1,0:T(8,128)} %param.10) | copy-start | bytes 98308
  43.5 3.6 %copy-start.6 = (f32[8,1024]{1,0:T(8,128)S(1)}, f32[8,1024]{1,0:T(8,128)}, u32[]{:S(2)}) copy-start(f32[8,1024]{1,0:T(8,128)} %param.11) | copy-start | bytes 98308
  47.1 1.3 %copy-start.1 = (f32[4096,128]{1,0:T(8,128)}, f32[4096,128]{1,0:T(8,128)S(1)}, u32[]{:S(2)}) copy-start(f32[4096,128]{1,0:T(8,128)S(1)} %scatter_custom_fusion) | copy-start | bytes 6291460

commit v2 on v1

v2 whole, which is shorter than its diff:
```python
import jax
import jax.numpy as jnp
from jax import lax
from jax.experimental import pallas as pl
from jax.experimental.pallas import tpu as pltpu
from jax.sharding import PartitionSpec as P

learn_rate = 0.5
max_norm = 8.0
epsilon = 1e-10
axes = ("gx", "gy")
lanes = 128


def swap(value, mask):
    count = lax.axis_size(axes)
    return lax.ppermute(value, axes, [(i, i ^ mask) for i in range(count)])


def pick(value, live, bits, flip):
    index = lax.axis_index(axes)
    for bit in bits:
        chosen = (index >> bit) & 1
        if (flip >> bit) & 1:
            chosen = 1 - chosen
        value = lax.dynamic_index_in_dim(value, chosen, live.index(bit), keepdims=False)
        live = [other for other in live if other != bit]
    return value


def masks_of(bits):
    return [sum(((code >> j) & 1) << bit for j, bit in enumerate(bits)) for code in range(1, 2 ** len(bits))]


def reduced(local_grad, touched, square, gather):
    count = lax.axis_size(axes)
    total_bits = count.bit_length() - 1
    own_rows = local_grad.shape[0] // count
    width = local_grad.shape[1]
    data = local_grad.reshape((2,) * total_bits + (own_rows, width))
    live = list(range(total_bits))[::-1]
    last = list(range(max(total_bits - 2, 3), total_bits))
    rounds = [[0], [1, 2]] + [[bit] for bit in range(3, last[0])]
    for bits in rounds:
        if len(bits) > 1:
            data, touched = lax.optimization_barrier((data, touched))
            row_square, square_table, embed_square = square(touched)
        arrived = [swap(pick(data, live, bits, mask), mask) for mask in masks_of(bits)[::-1]]
        data = pick(data, live, bits, 0)
        for part in arrived:
            data = data + part
        live = [bit for bit in live if bit not in bits]
    lead = data.shape[:-2]
    tile = jnp.zeros(lead + (own_rows, lanes), jnp.float32)
    tile = tile.at[(0,) * len(lead)].set(embed_square)
    data = jnp.concatenate([data, tile], axis=-1)
    for bit in last[:-1]:
        data = data + swap(data, 1 << bit)
    data, touched = lax.optimization_barrier((data, touched))
    gathered = gather(touched)
    data = data + swap(data, 1 << last[-1])
    copy, old_rows, old_acc = gathered
    data, old_rows = lax.optimization_barrier((data, old_rows))
    mean = data[..., :width] / jnp.float32(count)
    squares = jnp.sum(jnp.square(mean).reshape((-1, own_rows, width // lanes, lanes)), axis=(0, 2))
    partial = squares + data[..., width:][(0,) * len(lead)]
    for bits in rounds[::-1]:
        arrived = [swap(partial, mask) for mask in masks_of(bits)[::-1]]
        for part in arrived:
            partial = partial + part
    return pick(mean, live, live, 0), partial, (copy, old_rows, old_acc, row_square, square_table)


unroll = 8
pieces = 8


def square_kernel(touched, grads, row_square, square_table, embed_square):
    square = jnp.square(grads[...])
    embed_square[...] = jnp.sum(square.reshape((-1,) + embed_square.shape), axis=0)
    square_table[...] = jnp.zeros_like(square_table)
    total = jnp.sum(square, axis=1, keepdims=True)
    row_square[...] = jnp.broadcast_to(total / grads.shape[1], row_square.shape)
    lane = lax.broadcasted_iota(jnp.int32, (1, lanes), 1)

    def spread(step, _):
        base = pl.multiple_of(step * unroll, unroll)
        places = [touched[base + j] for j in range(unroll)]
        here = [lane == (place & (lanes - 1)) for place in places]
        values = [row_square[pl.ds(base + j, 1), :] for j in range(unroll)]
        for j in range(unroll):
            row = pl.ds(places[j] // lanes, 1)
            square_table[row, :] = jnp.where(here[j], values[j], square_table[row, :])
        return 0

    lax.fori_loop(0, grads.shape[0] // unroll, spread, 0)


def square_rows(touched, grads, table_rows):
    vmem = pl.BlockSpec(memory_space=pltpu.VMEM)
    return pl.pallas_call(
        square_kernel,
        out_shape=(
            pltpu.VMEM(grads.shape, jnp.float32),
            pltpu.VMEM((table_rows // lanes, lanes), jnp.float32),
            pltpu.VMEM((8, lanes), jnp.float32),
        ),
        in_specs=[pl.BlockSpec(memory_space=pltpu.SMEM), vmem],
        out_specs=(vmem,) * 3,
        name="square",
    )(touched, grads)


def gather_kernel(touched, table, row_acc, copy, old_rows, old_acc, held, loaded, stored):
    height = held.shape[0] // pieces
    parts = [pl.ds(k * height, height) for k in range(pieces)]
    loads = [pltpu.make_async_copy(table.at[part], held.at[part], loaded.at[k]) for k, part in enumerate(parts)]
    stores = [pltpu.make_async_copy(held.at[part], copy.at[part], stored.at[k]) for k, part in enumerate(parts)]
    for load in loads:
        load.start()
    lane = lax.broadcasted_iota(jnp.int32, (1, lanes), 1)

    def collect(step, _):
        base = pl.multiple_of(step * unroll, unroll)
        places = [touched[base + j] for j in range(unroll)]
        found = [row_acc[pl.ds(place // lanes, 1), :] for place in places]
        for j in range(unroll):
            old_acc[pl.ds(base + j, 1), :] = jnp.where(lane == (places[j] & (lanes - 1)), found[j], 0.0)
        return 0

    lax.fori_loop(0, old_acc.shape[0] // unroll, collect, 0)
    for load, store in zip(loads, stores):
        load.wait()
        store.start()
    chosen = jnp.sum(old_acc[...], axis=1, keepdims=True)
    old_acc[...] = jnp.broadcast_to(chosen, old_acc.shape)

    def gather(step, _):
        base = pl.multiple_of(step * unroll, unroll)
        rows = [held[pl.ds(touched[base + j], 1), :] for j in range(unroll)]
        for j in range(unroll):
            old_rows[pl.ds(base + j, 1), :] = rows[j]
        return 0

    lax.fori_loop(0, old_rows.shape[0] // unroll, gather, 0)
    for store in stores:
        store.wait()


def gather_rows(touched, table, row_acc):
    vmem = pl.BlockSpec(memory_space=pltpu.VMEM)
    any_space = pl.BlockSpec(memory_space=pl.ANY)
    return pl.pallas_call(
        gather_kernel,
        out_shape=(
            jax.ShapeDtypeStruct(table.shape, jnp.float32),
            pltpu.VMEM(touched.shape + table.shape[1:], jnp.float32),
            pltpu.VMEM(touched.shape + table.shape[1:], jnp.float32),
        ),
        in_specs=[pl.BlockSpec(memory_space=pltpu.SMEM), any_space, vmem],
        out_specs=(any_space, vmem, vmem),
        scratch_shapes=[
            pltpu.VMEM(table.shape, jnp.float32),
            pltpu.SemaphoreType.DMA((pieces,)),
            pltpu.SemaphoreType.DMA((pieces,)),
        ],
        name="gather",
    )(touched, table, pltpu.with_memory_space_constraint(row_acc, pltpu.VMEM))


def update_kernel(
    touched, partial, mean, param, acc, grads, old_rows, old_acc, row_square, square_table, row_acc, copy,
    new_param, new_acc, new_row_acc, new_table, rows, copied,
):
    norm_sq = jnp.sum(partial[...], keepdims=True)
    clip = jnp.minimum(jnp.float32(1.0), max_norm / (jnp.sqrt(norm_sq) + 1e-06))
    clip_sq = clip * clip
    updated = old_acc[...] + jnp.where(clip > 0, clip_sq * row_square[...], 0.0)
    rows[...] = old_rows[...] - learn_rate * (clip * grads[...]) / (jnp.sqrt(updated) + epsilon)

    def scatter(step, _):
        base = pl.multiple_of(step * unroll, unroll)
        for j in range(unroll):
            place = touched[base + j]
            pltpu.make_async_copy(rows.at[pl.ds(base + j, 1)], new_table.at[pl.ds(place, 1)], copied).start()
        return 0

    lax.fori_loop(0, grads.shape[0] // unroll, scatter, 0)
    scaled = clip * mean[...]
    grown = acc[...] + scaled * scaled
    new_acc[...] = grown
    new_param[...] = param[...] - learn_rate * scaled / (jnp.sqrt(grown) + epsilon)
    new_row_acc[...] = row_acc[...] + jnp.where(clip > 0, clip_sq * square_table[...], 0.0)
    pltpu.make_async_copy(rows, new_table.at[pl.ds(0, rows.shape[0])], copied).wait()


def update(touched, partial, mean, param, acc, grads, prepared, row_acc):
    copy = prepared[0]
    old_rows, old_acc, row_square, square_table = [
        pltpu.with_memory_space_constraint(value, pltpu.VMEM) for value in prepared[1:]
    ]
    vmem = pl.BlockSpec(memory_space=pltpu.VMEM)
    any_space = pl.BlockSpec(memory_space=pl.ANY)
    return pl.pallas_call(
        update_kernel,
        out_shape=(
            jax.ShapeDtypeStruct(param.shape, jnp.float32),
            jax.ShapeDtypeStruct(acc.shape, jnp.float32),
            jax.ShapeDtypeStruct(row_acc.shape, jnp.float32),
            jax.ShapeDtypeStruct(copy.shape, jnp.float32),
        ),
        in_specs=[pl.BlockSpec(memory_space=pltpu.SMEM)] + [vmem] * 10 + [any_space],
        out_specs=(vmem, vmem, vmem, any_space),
        input_output_aliases={11: 3},
        scratch_shapes=[pltpu.VMEM(grads.shape, jnp.float32), pltpu.SemaphoreType.DMA],
        name="update",
    )(touched, partial, mean, param, acc, grads, old_rows, old_acc, row_square, square_table, row_acc, copy)


def body(dense_grads, dense_param, dense_acc, table, row_acc, touched, emb_grads):
    flat_acc = row_acc.reshape((-1, lanes))
    mean_grad, partial, prepared = reduced(
        dense_grads[0],
        touched,
        lambda places: square_rows(places, emb_grads, row_acc.shape[0]),
        lambda places: gather_rows(places, table, flat_acc),
    )
    close = [
        pltpu.with_memory_space_constraint(value, pltpu.VMEM)
        for value in (partial, mean_grad, dense_param, dense_acc, emb_grads)
    ]
    new_dense, new_dense_acc, new_row_acc, new_table = update(
        touched, *close, prepared, pltpu.with_memory_space_constraint(flat_acc, pltpu.VMEM)
    )
    return (new_dense, new_dense_acc, new_table, new_row_acc.reshape(row_acc.shape))


def solution(mesh):
    return jax.shard_map(
        body,
        mesh=mesh,
        in_specs=(
            P(axes, None, None),
            P(axes, None),
            P(axes, None),
            P(axes, None),
            P(axes),
            P(axes),
            P(axes, None),
        ),
        out_specs=(P(axes, None), P(axes, None), P(axes, None), P(axes)),
        check_vma=False,
    )
```

time: 48.6 us -> 41.4 us (0.85)
  Pallas kernels: 0 us -> 13.4 us
  waiting for transfers between devices: 21.3 us -> 12.3 us
  local copies, waits for them, and re-layouts: 7.6 us -> 1.43 us
  other arithmetic: 5.96 us -> 0.19 us
  starting transfers between devices: 12.1 us -> 13.1 us
  between operations: 1.58 us -> 0.79 us
    pallas_call x0 -> x3, Pallas kernels: none -> 13.4 us  [the longest x1 5.21 us: gather_rows(): pl.pallas_call(gather_kernel, out_shape=(jax.ShapeDtypeStruct(table.shape...]
    ppermute x9 -> x10, waiting for transfers between devices: 21.3 us -> 12.3 us  [swap(): return lax.ppermute(value, axes, [(i, i ^ mask) for i in range(count)])]
    scatter x1 -> x0, other arithmetic: 3.6 us -> none  [body(): new_table = table.at[touched].set(updated_rows, unique_indices=True)]
    gather x1 -> x0, local copies, waits for them, and re-layouts: 3.14 us -> none  [body(): old_acc = row_acc[touched]]
    scatter x1 -> x0, local copies, waits for them, and re-layouts: 2.46 us -> none  [body(): jnp.zeros_like(row_acc).at[touched].set(row_square, unique_indices=True)]
    unnamed x16 -> x8, local copies, waits for them, and re-layouts: 1.81 us -> 0.03 us
    dynamic_slice x2, local copies, waits for them, and re-layouts: 0.14 us -> 1.35 us  [pick(): lax.dynamic_index_in_dim(value, chosen, live.index(bit), keepdims=False)]
    ppermute x9 -> x10, starting transfers between devices: 12.1 us -> 13.1 us  [swap(): return lax.ppermute(value, axes, [(i, i ^ mask) for i in range(count)])]
  transfers between devices with their start and end apart: 9 -> 10, of which waited for: 8 -> 9; matrix products, arithmetic and copies ran while one was open for 7% -> 0% of each run, Pallas kernels for 0% -> 23%
where the time goes in v2:
time: 41.4 us; the launch traced here: 41.2 us
  Pallas kernels  13.4 us (32%)
  starting transfers between devices  13.1 us (32%)
  waiting for transfers between devices  12.3 us (30%)
  local copies, waits for them, and re-layouts  1.43 us (3%)
  between operations  0.79 us (2%)
    ppermute x10, starting transfers between devices, swap(): return lax.ppermute(value, axes, [(i, i ^ mask) for i in range(count)])  13.1 us
    ppermute x10, waiting for transfers between devices, swap(): return lax.ppermute(value, axes, [(i, i ^ mask) for i in range(count)])  12.3 us
    pallas_call x1, Pallas kernels, gather_rows(): pl.pallas_call(gather_kernel, out_shape=(jax.ShapeDtypeStruct(table.shape...  5.21 us
    pallas_call x1, Pallas kernels, square_rows(): pl.pallas_call(square_kernel, out_shape=(pltpu.VMEM(grads.shape, jnp.floa...  4.19 us
    pallas_call x1, Pallas kernels, update(): pl.pallas_call(update_kernel, out_shape=(jax.ShapeDtypeStruct(param.shape...  4.02 us
    dynamic_slice x2, local copies, waits for them, and re-layouts, pick(): lax.dynamic_index_in_dim(value, chosen, live.index(bit), keepdims=False)  1.35 us
  transfers between devices with their start and end apart: 10, of which 9 were waited for; matrix products, arithmetic and copies ran while one was open for 0% of the time, Pallas kernels for 23%

profile of v2, /device:TPU:0, one launch (start us, length us, event | category | flops | bytes accessed | tf_op | source)
XLA Modules:
  0.0 41.2 jit_solution(3364396188968665542)
XLA Ops:
  0.6 1.3 %constant_dynamic-slice_fusion.1 = (f32[2,2,2,2,1,8,1024]{6,5,4,3,2,1,0:T(8,128)S(1)}, f32[2,2,2,2,1,8,1024]{6,5,4,3,2,1,0:T(8,128)S(1)}) fusion(f32[2,2,2,2,2,8,1024]{6,5,4,3,2,1,0:T(8,128)} %bitcast.31, s32[]{:T(128)S(6)} %select_n.45, s32[]{:T(128)S(6)} %select_n.46), kind=kLoop, calls=%fused_computation.17 | loop fusion | bytes 2097160 | tf_op jit(solution)/shard_map/jit(dynamic_index_in_dim)/dynamic_slice | solution.py:26
  2.0 0.6 %collective-permute-start = (f32[2,2,2,2,8,1024]{5,4,1,0,3,2:T(8,128)S(1)}, f32[2,2,2,2,8,1024]{5,4,1,0,3,2:T(8,128)S(1)}, u32[]{:S(2)}, u32[]{:S(2)}) collective-permute-start(f32[2,2,2,2,8,1024]{5,4,1,0,3,2:T(8,128)S(1)} %bitcast.32), channel_id=1, source_target_pairs={{0,1},{1,0},{2,3},{3,2},{4,5},{5,4},{6,7},{7,6},{8,9},{9,8},{10,11... | collective-permute-start | bytes 1572872 | tf_op jit(solution)/shard_map/ppermute | solution.py:17
  2.6 1.5 %collective-permute-done = f32[2,2,2,2,8,1024]{5,4,1,0,3,2:T(8,128)S(1)} collective-permute-done((f32[2,2,2,2,8,1024]{5,4,1,0,3,2:T(8,128)S(1)}, f32[2,2,2,2,8,1024]{5,4,1,0,3,2:T(8,128)S(1)}, u32[]{:S(2)}, u32[]{:S(2)}) %collective-permute-start) | collective-permute-done | bytes 524320 | tf_op jit(solution)/shard_map/ppermute | solution.py:17
  4.1 0.1 bitcast_add_fusion
  4.2 3.9 %collective-permute-start.1 = (f32[2,2,8,1024]{3,2,1,0:T(8,128)S(1)}, f32[2,2,8,1024]{3,2,1,0:T(8,128)S(1)}, u32[]{:S(2)}, u32[]{:S(2)}) collective-permute-start(f32[2,2,8,1024]{3,2,1,0:T(8,128)S(1)} %get-tuple-element.50), channel_id=1, source_target_pairs={{0,6},{1,7},{2,4},{3,5},{4,2},{5,3},{6,0},{7,1},{8,14},{9,15},{10,... | collective-permute-start | bytes 393224 | tf_op jit(solution)/shard_map/ppermute | solution.py:17
  8.1 0.5 %collective-permute-start.3 = (f32[2,2,8,1024]{3,2,1,0:T(8,128)S(1)}, f32[2,2,8,1024]{3,2,1,0:T(8,128)S(1)}, u32[]{:S(2)}, u32[]{:S(2)}) collective-permute-start(f32[2,2,8,1024]{3,2,1,0:T(8,128)S(1)} %get-tuple-element.51), channel_id=1, source_target_pairs={{0,2},{1,3},{2,0},{3,1},{4,6},{5,7},{6,4},{7,5},{8,10},{9,11},{10,... | collective-permute-start | bytes 393224 | tf_op jit(solution)/shard_map/ppermute | solution.py:17
  8.6 0.1 collective-permute-start.2
  8.7 4.2 %square.6 = (f32[512,128]{1,0:T(8,128)S(1)}, f32[32,128]{1,0:T(8,128)S(1)}, f32[8,128]{1,0:T(8,128)S(1)}) custom-call(s32[512]{0:T(512)} %touched.3, f32[512,128]{1,0:T(8,128)} %grads.3), custom_call_target="tpu_custom_call" | custom-call | tf_op jit(solution)/shard_map/square/pallas_call | solution.py:101
  12.9 0.0 copy-start
  12.9 0.0 copy-start.2
  13.0 1.7 %collective-permute-done.3 = f32[2,2,8,1024]{3,2,1,0:T(8,128)S(1)} collective-permute-done((f32[2,2,8,1024]{3,2,1,0:T(8,128)S(1)}, f32[2,2,8,1024]{3,2,1,0:T(8,128)S(1)}, u32[]{:S(2)}, u32[]{:S(2)}) %collective-permute-start.3) | collective-permute-done | bytes 131104 | tf_op jit(solution)/shard_map/ppermute | solution.py:17
  14.7 0.3 collective-permute-done.2
  15.0 1.6 %collective-permute-start.4 = (f32[2,2,8,1152]{3,2,1,0:T(8,128)S(1)}, f32[2,2,8,1152]{3,2,1,0:T(8,128)S(1)}, u32[]{:S(2)}, u32[]{:S(2)}) collective-permute-start(f32[2,2,8,1152]{3,2,1,0:T(8,128)S(1)} %select_maximum_fusion), channel_id=1, source_target_pairs={{0,8},{1,9},{2,10},{3,11},{4,12},{5,13},{6,14},{7,15},{8,0},{9,1},... | collective-permute-start | bytes 442376 | tf_op jit(solution)/shard_map/ppermute | solution.py:17
  16.7 3.9 %collective-permute-done.4 = f32[2,2,8,1152]{3,2,1,0:T(8,128)S(1)} collective-permute-done((f32[2,2,8,1152]{3,2,1,0:T(8,128)S(1)}, f32[2,2,8,1152]{3,2,1,0:T(8,128)S(1)}, u32[]{:S(2)}, u32[]{:S(2)}) %collective-permute-start.4) | collective-permute-done | bytes 147488 | tf_op jit(solution)/shard_map/ppermute | solution.py:17
  20.6 2.8 %collective-permute-start.5 = (f32[2,2,8,1152]{3,2,1,0:T(8,128)S(1)}, f32[2,2,8,1152]{3,2,1,0:T(8,128)S(1)}, u32[]{:S(2)}, u32[]{:S(2)}) collective-permute-start(f32[2,2,8,1152]{3,2,1,0:T(8,128)S(1)} %fusion.2), channel_id=1, source_target_pairs={{0,16},{1,17},{2,18},{3,19},{4,20},{5,21},{6,22},{7,23},{8,24},{9,... | collective-permute-start | bytes 442376 | tf_op jit(solution)/shard_map/ppermute | solution.py:17
  23.5 5.2 %gather.1 = (f32[4096,128]{1,0:T(8,128)}, f32[512,128]{1,0:T(8,128)S(1)}, f32[512,128]{1,0:T(8,128)S(1)}) custom-call(s32[512]{0:T(512)} %touched.3, f32[4096,128]{1,0:T(8,128)} %table.1, f32[32,128]{1,0:T(8,128)S(1)} %bitcast.27), custom_call_target="tpu_custom_call" | custom-call | tf_op jit(solution)/shard_map/gather/pallas_call | solution.py:153
  28.7 1.0 %collective-permute-done.5 = f32[2,2,8,1152]{3,2,1,0:T(8,128)S(1)} collective-permute-done((f32[2,2,8,1152]{3,2,1,0:T(8,128)S(1)}, f32[2,2,8,1152]{3,2,1,0:T(8,128)S(1)}, u32[]{:S(2)}, u32[]{:S(2)}) %collective-permute-start.5) | collective-permute-done | bytes 147488 | tf_op jit(solution)/shard_map/ppermute | solution.py:17
  29.8 1.7 %collective-permute-start.8 = (f32[8,128]{1,0:T(8,128)S(1)}, f32[8,128]{1,0:T(8,128)S(1)}, u32[]{:S(2)}, u32[]{:S(2)}) collective-permute-start(f32[8,128]{1,0:T(8,128)S(1)} %bitcast_add_fusion.2), channel_id=1, source_target_pairs={{0,2},{1,3},{2,0},{3,1},{4,6},{5,7},{6,4},{7,5},{8,10},{9,11},{10,... | collective-permute-start | bytes 12296 | tf_op jit(solution)/shard_map/ppermute | solution.py:17
  31.5 1.8 %collective-permute-start.6 = (f32[8,128]{1,0:T(8,128)S(1)}, f32[8,128]{1,0:T(8,128)S(1)}, u32[]{:S(2)}, u32[]{:S(2)}) collective-permute-start(f32[8,128]{1,0:T(8,128)S(1)} %bitcast_add_fusion.2), channel_id=1, source_target_pairs={{0,6},{1,7},{2,4},{3,5},{4,2},{5,3},{6,0},{7,1},{8,14},{9,15},{10,... | collective-permute-start | bytes 12296 | tf_op jit(solution)/shard_map/ppermute | solution.py:17
  33.3 0.1 collective-permute-done.8
  33.5 1.7 %collective-permute-done.7 = f32[8,128]{1,0:T(8,128)S(1)} collective-permute-done((f32[8,128]{1,0:T(8,128)S(1)}, f32[8,128]{1,0:T(8,128)S(1)}, u32[]{:S(2)}, u32[]{:S(2)}) %collective-permute-start.7) | collective-permute-done | bytes 4128 | tf_op jit(solution)/shard_map/ppermute | solution.py:17
  35.1 0.9 %collective-permute-done.6 = f32[8,128]{1,0:T(8,128)S(1)} collective-permute-done((f32[8,128]{1,0:T(8,128)S(1)}, f32[8,128]{1,0:T(8,128)S(1)}, u32[]{:S(2)}, u32[]{:S(2)}) %collective-permute-start.6) | collective-permute-done | bytes 4128 | tf_op jit(solution)/shard_map/ppermute | solution.py:17
  36.1 1.1 %collective-permute-done.9 = f32[8,128]{1,0:T(8,128)S(1)} collective-permute-done((f32[8,128]{1,0:T(8,128)S(1)}, f32[8,128]{1,0:T(8,128)S(1)}, u32[]{:S(2)}, u32[]{:S(2)}) %collective-permute-start.9) | collective-permute-done | bytes 4128 | tf_op jit(solution)/shard_map/ppermute | solution.py:17
  37.2 4.0 %update.1 = (f32[8,1024]{1,0:T(8,128)}, f32[8,1024]{1,0:T(8,128)}, f32[32,128]{1,0:T(8,128)}, f32[4096,128]{1,0:T(8,128)}) custom-call(s32[512]{0:T(512)} %touched.3, f32[8,128]{1,0:T(8,128)S(1)} %add.127.partial, f32[8,1024]{1,0:T(8,128)S(1)} %dynamic-slice_bitcast_fusion.3.mean, f32[8,1024]{1,0:T(8,128)S(1)} %copy-done.2, ...), custom_call_target="tpu_custom_call", output_to_operand_aliasing={{3}: (11, {})} | custom-call | tf_op jit(solution)/shard_map/update/pallas_call | solution.py:204
  (21 shorter events, 0.3 us)
Async XLA Ops:
  2.0 21.5 %copy-start.1 = (f32[4096]{0:T(1024)S(1)}, f32[4096]{0:T(1024)}, u32[]{:S(2)}) copy-start(f32[4096]{0:T(1024)} %param.14) | copy-start | bytes 49156
  2.0 2.1 %collective-permute-start = (f32[2,2,2,2,8,1024]{5,4,1,0,3,2:T(8,128)S(1)}, f32[2,2,2,2,8,1024]{5,4,1,0,3,2:T(8,128)S(1)}, u32[]{:S(2)}, u32[]{:S(2)}) collective-permute-start(f32[2,2,2,2,8,1024]{5,4,1,0,3,2:T(8,128)S(1)} %bitcast.32), channel_id=1, source_target_pairs={{0,1},{1,0},{2,3},{3,2},{4,5},{5,4},{6,7},{7,6},{8,9},{9,8},{10,11... | collective-permute-start | bytes 1572872 | tf_op jit(solution)/shard_map/ppermute | solution.py:17
  4.2 8.8 %collective-permute-start.1 = (f32[2,2,8,1024]{3,2,1,0:T(8,128)S(1)}, f32[2,2,8,1024]{3,2,1,0:T(8,128)S(1)}, u32[]{:S(2)}, u32[]{:S(2)}) collective-permute-start(f32[2,2,8,1024]{3,2,1,0:T(8,128)S(1)} %get-tuple-element.50), channel_id=1, source_target_pairs={{0,6},{1,7},{2,4},{3,5},{4,2},{5,3},{6,0},{7,1},{8,14},{9,15},{10,... | collective-permute-start | bytes 393224 | tf_op jit(solution)/shard_map/ppermute | solution.py:17
  8.1 6.6 %collective-permute-start.3 = (f32[2,2,8,1024]{3,2,1,0:T(8,128)S(1)}, f32[2,2,8,1024]{3,2,1,0:T(8,128)S(1)}, u32[]{:S(2)}, u32[]{:S(2)}) collective-permute-start(f32[2,2,8,1024]{3,2,1,0:T(8,128)S(1)} %get-tuple-element.51), channel_id=1, source_target_pairs={{0,2},{1,3},{2,0},{3,1},{4,6},{5,7},{6,4},{7,5},{8,10},{9,11},{10,... | collective-permute-start | bytes 393224 | tf_op jit(solution)/shard_map/ppermute | solution.py:17
  8.6 6.4 %collective-permute-start.2 = (f32[2,2,8,1024]{3,2,1,0:T(8,128)S(1)}, f32[2,2,8,1024]{3,2,1,0:T(8,128)S(1)}, u32[]{:S(2)}, u32[]{:S(2)}) collective-permute-start(f32[2,2,8,1024]{3,2,1,0:T(8,128)S(1)} %get-tuple-element.52), channel_id=1, source_target_pairs={{0,4},{1,5},{2,6},{3,7},{4,0},{5,1},{6,2},{7,3},{8,12},{9,13},{10,... | collective-permute-start | bytes 393224 | tf_op jit(solution)/shard_map/ppermute | solution.py:17
  12.9 24.3 %copy-start = (f32[512,128]{1,0:T(8,128)S(1)}, f32[512,128]{1,0:T(8,128)}, u32[]{:S(2)}) copy-start(f32[512,128]{1,0:T(8,128)} %grads.3) | copy-start | bytes 786436
  12.9 24.3 %copy-start.2 = (f32[8,1024]{1,0:T(8,128)S(1)}, f32[8,1024]{1,0:T(8,128)}, u32[]{:S(2)}) copy-start(f32[8,1024]{1,0:T(8,128)} %param.17) | copy-start | bytes 98308
  13.0 24.2 %copy-start.3 = (f32[8,1024]{1,0:T(8,128)S(1)}, f32[8,1024]{1,0:T(8,128)}, u32[]{:S(2)}) copy-start(f32[8,1024]{1,0:T(8,128)} %acc.1) | copy-start | bytes 98308
  15.0 5.6 %collective-permute-start.4 = (f32[2,2,8,1152]{3,2,1,0:T(8,128)S(1)}, f32[2,2,8,1152]{3,2,1,0:T(8,128)S(1)}, u32[]{:S(2)}, u32[]{:S(2)}) collective-permute-start(f32[2,2,8,1152]{3,2,1,0:T(8,128)S(1)} %select_maximum_fusion), channel_id=1, source_target_pairs={{0,8},{1,9},{2,10},{3,11},{4,12},{5,13},{6,14},{7,15},{8,0},{9,1},... | collective-permute-start | bytes 442376 | tf_op jit(solution)/shard_map/ppermute | solution.py:17
  20.6 9.1 %collective-permute-start.5 = (f32[2,2,8,1152]{3,2,1,0:T(8,128)S(1)}, f32[2,2,8,1152]{3,2,1,0:T(8,128)S(1)}, u32[]{:S(2)}, u32[]{:S(2)}) collective-permute-start(f32[2,2,8,1152]{3,2,1,0:T(8,128)S(1)} %fusion.2), channel_id=1, source_target_pairs={{0,16},{1,17},{2,18},{3,19},{4,20},{5,21},{6,22},{7,23},{8,24},{9,... | collective-permute-start | bytes 442376 | tf_op jit(solution)/shard_map/ppermute | solution.py:17
  29.8 3.7 %collective-permute-start.8 = (f32[8,128]{1,0:T(8,128)S(1)}, f32[8,128]{1,0:T(8,128)S(1)}, u32[]{:S(2)}, u32[]{:S(2)}) collective-permute-start(f32[8,128]{1,0:T(8,128)S(1)} %bitcast_add_fusion.2), channel_id=1, source_target_pairs={{0,2},{1,3},{2,0},{3,1},{4,6},{5,7},{6,4},{7,5},{8,10},{9,11},{10,... | collective-permute-start | bytes 12296 | tf_op jit(solution)/shard_map/ppermute | solution.py:17
  31.5 3.6 %collective-permute-start.7 = (f32[8,128]{1,0:T(8,128)S(1)}, f32[8,128]{1,0:T(8,128)S(1)}, u32[]{:S(2)}, u32[]{:S(2)}) collective-permute-start(f32[8,128]{1,0:T(8,128)S(1)} %bitcast_add_fusion.2), channel_id=1, source_target_pairs={{0,4},{1,5},{2,6},{3,7},{4,0},{5,1},{6,2},{7,3},{8,12},{9,13},{10,... | collective-permute-start | bytes 12296 | tf_op jit(solution)/shard_map/ppermute | solution.py:17
  31.5 4.5 %collective-permute-start.6 = (f32[8,128]{1,0:T(8,128)S(1)}, f32[8,128]{1,0:T(8,128)S(1)}, u32[]{:S(2)}, u32[]{:S(2)}) collective-permute-start(f32[8,128]{1,0:T(8,128)S(1)} %bitcast_add_fusion.2), channel_id=1, source_target_pairs={{0,6},{1,7},{2,4},{3,5},{4,2},{5,3},{6,0},{7,1},{8,14},{9,15},{10,... | collective-permute-start | bytes 12296 | tf_op jit(solution)/shard_map/ppermute | solution.py:17
  36.0 1.2 %collective-permute-start.9 = (f32[8,128]{1,0:T(8,128)S(1)}, f32[8,128]{1,0:T(8,128)S(1)}, u32[]{:S(2)}, u32[]{:S(2)}) collective-permute-start(f32[8,128]{1,0:T(8,128)S(1)} %add_add_fusion), channel_id=1, source_target_pairs={{0,1},{1,0},{2,3},{3,2},{4,5},{5,4},{6,7},{7,6},{8,9},{9,8},{10,11... | collective-permute-start | bytes 12296 | tf_op jit(solution)/shard_map/ppermute | solution.py:17
